TPU v7x, 16 devices: a whole 2x2x2 slice. The times are simulated.
16 devices in a mesh: fsdp: 16 (over z, y, x, core).
Axes of the slice: x: 2, y: 2, z: 2, core: 2. Of those that a mesh axis runs over, the one named last changes fastest.
Arguments:
- tokens: int32 [16, 2048], P('fsdp')
- positions: int32 [16, 2048], P('fsdp')
- tok_table: float32 [49152, 768], P('fsdp')
- pos_table: float32 [8192, 768], P('fsdp')
- ln1_gain: float32 [768], P('fsdp')
- ln1_bias: float32 [768], P('fsdp')
- w_qkv: float32 [768, 896], P('fsdp')
- b_qkv: float32 [896], P('fsdp')
- w_out: float32 [768, 768], P('fsdp')
- b_out: float32 [768], P('fsdp')
- ln2_gain: float32 [768], P('fsdp')
- ln2_bias: float32 [768], P('fsdp')
- w_fc: float32 [768, 3072], P('fsdp')
- b_fc: float32 [3072], P('fsdp')
- w_proj: float32 [3072, 768], P('fsdp')
- b_proj: float32 [768], P('fsdp')
- grad_out: bfloat16 [16, 2048, 768], P('fsdp')
Outputs:
- output 1: bfloat16 [16, 2048, 768], P('fsdp')
- output 2: float32 [49152, 768], P('fsdp')
- output 3: float32 [8192, 768], P('fsdp')
- output 4: float32 [768], P('fsdp')
- output 5: float32 [768], P('fsdp')
- output 6: float32 [768, 896], P('fsdp')
- output 7: float32 [896], P('fsdp')
- output 8: float32 [768, 768], P('fsdp')
- output 9: float32 [768], P('fsdp')
- output 10: float32 [768], P('fsdp')
- output 11: float32 [768], P('fsdp')
- output 12: float32 [768, 3072], P('fsdp')
- output 13: float32 [3072], P('fsdp')
- output 14: float32 [3072, 768], P('fsdp')
- output 15: float32 [768], P('fsdp')
All inputs are finite; a program needn't handle non-finite values.
Results may differ from a plain program's by a relative error of at most 0.02.
Values are sent between devices in bfloat16 or wider.
A program may use at most 1 GiB of HBM per device.

v0:
```python
import jax
import jax.numpy as jnp
from jax import lax
from jax.sharding import PartitionSpec as P


def layer_norm(rows_in, ln_gain, ln_shift):
    row_mean = jnp.mean(rows_in, axis=-1, keepdims=True)
    centered = rows_in - row_mean
    row_var = jnp.mean(centered * centered, axis=-1, keepdims=True)
    return centered * lax.rsqrt(row_var + 1e-5) * ln_gain + ln_shift


def gelu_tanh(pre_act):
    return jax.nn.gelu(pre_act, approximate=True)


def layer_pass(x_emb, grad_out, weights):
    (ln1_gain, ln1_bias, w_qkv, b_qkv, w_out, b_out, ln2_gain, ln2_bias, w_fc, b_fc, w_proj, b_proj) = weights
    batch_dim, seq_len, model_dim = x_emb.shape
    head_dim = (w_qkv.shape[1] - model_dim) // 2
    num_heads = model_dim // head_dim
    score_scale = head_dim ** -0.5
    x_res = x_emb.astype(jnp.float32)
    ln1_out, pull_ln1 = jax.vjp(layer_norm, x_res, ln1_gain.astype(jnp.float32), ln1_bias.astype(jnp.float32))
    ln1_act = ln1_out.astype(jnp.bfloat16)
    qkv_act = (jnp.einsum('bsd,de->bse', ln1_act, w_qkv, preferred_element_type=jnp.float32) + b_qkv.astype(jnp.float32)).astype(jnp.bfloat16)
    query_heads = qkv_act[:, :, :model_dim].reshape(batch_dim, seq_len, num_heads, head_dim)
    key_head = qkv_act[:, :, model_dim:model_dim + head_dim]
    value_head = qkv_act[:, :, model_dim + head_dim:]
    scores = jnp.einsum('bshd,btd->bhst', query_heads, key_head, preferred_element_type=jnp.float32) * score_scale
    causal = jnp.arange(seq_len)[:, None] >= jnp.arange(seq_len)[None, :]
    attn_prob = jax.nn.softmax(jnp.where(causal, scores, -1e30), axis=-1)
    prob_lo = attn_prob.astype(jnp.bfloat16)
    context = jnp.einsum('bhst,btd->bshd', prob_lo, value_head, preferred_element_type=jnp.float32).astype(jnp.bfloat16).reshape(batch_dim, seq_len, model_dim)
    attn_out = jnp.einsum('bsd,de->bse', context, w_out, preferred_element_type=jnp.float32) + b_out.astype(jnp.float32)
    hidden1 = (x_res + attn_out).astype(jnp.bfloat16)
    h1_wide = hidden1.astype(jnp.float32)
    ln2_out, pull_ln2 = jax.vjp(layer_norm, h1_wide, ln2_gain.astype(jnp.float32), ln2_bias.astype(jnp.float32))
    ln2_act = ln2_out.astype(jnp.bfloat16)
    pre_fc = (jnp.einsum('bsd,df->bsf', ln2_act, w_fc, preferred_element_type=jnp.float32) + b_fc.astype(jnp.float32)).astype(jnp.bfloat16)
    gelu_val, pull_gelu = jax.vjp(gelu_tanh, pre_fc.astype(jnp.float32))
    act_fc = gelu_val.astype(jnp.bfloat16)
    mlp_out = jnp.einsum('bsf,fd->bsd', act_fc, w_proj, preferred_element_type=jnp.float32) + b_proj.astype(jnp.float32)
    hidden_out = (h1_wide + mlp_out).astype(jnp.bfloat16)

    dy_wide = grad_out.astype(jnp.float32)
    g_b_proj = jnp.sum(dy_wide, axis=(0, 1))
    g_w_proj = jnp.einsum('bsf,bsd->fd', act_fc, grad_out, preferred_element_type=jnp.float32)
    d_act_fc = jnp.einsum('bsd,fd->bsf', grad_out, w_proj, preferred_element_type=jnp.float32).astype(jnp.bfloat16)
    d_pre_fc = pull_gelu(d_act_fc.astype(jnp.float32))[0].astype(jnp.bfloat16)
    g_b_fc = jnp.sum(d_pre_fc, axis=(0, 1), dtype=jnp.float32)
    g_w_fc = jnp.einsum('bsd,bsf->df', ln2_act, d_pre_fc, preferred_element_type=jnp.float32)
    d_ln2_act = jnp.einsum('bsf,df->bsd', d_pre_fc, w_fc, preferred_element_type=jnp.float32).astype(jnp.bfloat16)
    d_h1_norm, g_ln2_gain, g_ln2_bias = pull_ln2(d_ln2_act.astype(jnp.float32))
    d_hidden1 = (dy_wide + d_h1_norm).astype(jnp.bfloat16)
    g_b_out = jnp.sum(d_hidden1, axis=(0, 1), dtype=jnp.float32)
    g_w_out = jnp.einsum('bsd,bse->de', context, d_hidden1, preferred_element_type=jnp.float32)
    d_context = jnp.einsum('bse,de->bsd', d_hidden1, w_out, preferred_element_type=jnp.float32).astype(jnp.bfloat16).reshape(batch_dim, seq_len, num_heads, head_dim)
    d_prob = jnp.einsum('bshd,btd->bhst', d_context, value_head, preferred_element_type=jnp.float32).astype(jnp.bfloat16).astype(jnp.float32)
    d_value = jnp.einsum('bhst,bshd->btd', prob_lo, d_context, preferred_element_type=jnp.float32)
    weighted = jnp.sum(attn_prob * d_prob, axis=-1, keepdims=True)
    d_scores = (attn_prob * (d_prob - weighted) * score_scale).astype(jnp.bfloat16)
    d_query = jnp.einsum('bhst,btd->bshd', d_scores, key_head, preferred_element_type=jnp.float32).reshape(batch_dim, seq_len, model_dim)
    d_key = jnp.einsum('bhst,bshd->btd', d_scores, query_heads, preferred_element_type=jnp.float32)
    d_qkv = jnp.concatenate([d_query, d_key, d_value], axis=-1).astype(jnp.bfloat16)
    g_b_qkv = jnp.sum(d_qkv, axis=(0, 1), dtype=jnp.float32)
    g_w_qkv = jnp.einsum('bsd,bse->de', ln1_act, d_qkv, preferred_element_type=jnp.float32)
    d_ln1_act = jnp.einsum('bse,de->bsd', d_qkv, w_qkv, preferred_element_type=jnp.float32).astype(jnp.bfloat16)
    d_x_norm, g_ln1_gain, g_ln1_bias = pull_ln1(d_ln1_act.astype(jnp.float32))
    d_x0 = d_hidden1.astype(jnp.float32) + d_x_norm
    layer_grads = (g_ln1_gain, g_ln1_bias, g_w_qkv, g_b_qkv, g_w_out, g_b_out, g_ln2_gain, g_ln2_bias, g_w_fc, g_b_fc, g_w_proj, g_b_proj)
    return hidden_out, d_x0, layer_grads


def gather_rows(row_shard):
    return lax.all_gather(row_shard.astype(jnp.bfloat16), 'fsdp', axis=0, tiled=True)


def scatter_sum(dense_grad):
    return lax.psum_scatter(dense_grad, 'fsdp', scatter_dimension=0, tiled=True)


def solution(mesh):
    vec_spec = P('fsdp')
    mat_spec = P('fsdp', None)
    act_spec = P('fsdp', None, None)
    param_specs = (vec_spec, vec_spec, mat_spec, vec_spec, mat_spec, vec_spec, vec_spec, vec_spec, mat_spec, vec_spec, mat_spec, vec_spec)
    in_specs = (mat_spec, mat_spec, mat_spec, mat_spec) + param_specs + (act_spec,)
    out_specs = (act_spec, mat_spec, mat_spec) + param_specs

    def device_body(tokens, positions, tok_table, pos_table, ln1_gain, ln1_bias, w_qkv, b_qkv, w_out, b_out, ln2_gain, ln2_bias, w_fc, b_fc, w_proj, b_proj, grad_out):
        tok_full = gather_rows(tok_table)
        pos_full = gather_rows(pos_table)
        weights = tuple(gather_rows(master) for master in (ln1_gain, ln1_bias, w_qkv, b_qkv, w_out, b_out, ln2_gain, ln2_bias, w_fc, b_fc, w_proj, b_proj))
        tok_rows = jnp.take(tok_full, tokens, axis=0)
        pos_rows = jnp.take(pos_full, positions, axis=0)
        x_emb = (tok_rows.astype(jnp.float32) + pos_rows.astype(jnp.float32)).astype(jnp.bfloat16)
        hidden_out, d_x0, layer_grads = layer_pass(x_emb, grad_out, weights)
        flat_dx = d_x0.reshape(-1, d_x0.shape[-1])
        g_tok = scatter_sum(jax.ops.segment_sum(flat_dx, tokens.reshape(-1), num_segments=tok_full.shape[0]))
        g_pos = scatter_sum(jax.ops.segment_sum(flat_dx, positions.reshape(-1), num_segments=pos_full.shape[0]))
        return (hidden_out, g_tok, g_pos) + tuple(scatter_sum(layer_grad) for layer_grad in layer_grads)

    return jax.shard_map(device_body, mesh=mesh, in_specs=in_specs, out_specs=out_specs, check_vma=False)
```

profile of v0, /device:TPU:0, one launch (start us, length us, event | category | flops | bytes accessed | tf_op | source)
XLA Modules:
  0.0 2218.5 jit_solution(17940769941181676372)
XLA Ops:
  27.4 35.9 %all-reduce.17 = (bf16[768]{0:T(1024)(128)(2,1)}, bf16[896]{0:T(1024)(128)(2,1)S(1)}, bf16[768]{0:T(1024)(128)(2,1)S(1)}, bf16[768]{0:T(1024)(128)(2,1)S(1)}, bf...) all-reduce(bf16[768]{0:T(1024)(128)(2,1)S(1)} %dynamic-update-slice, ...), channel_id=1, replica_groups=mesh['fsdp'=16] {'fsdp'}, use_global_device_ids=true, to_apply=%add.7 | all-reduce | flops 8576 | bytes 34304
  68.8 8.6 all-gather.9.cloned.1.call-done
  77.4 14.7 gather_fusion.1
  94.9 254.6 %all-gather.7.cloned.1.call-done = bf16[49152,768]{1,0:T(8,128)(2,1)} async-done(((bf16[3072,768]{1,0:T(8,128)(2,1)}), bf16[49152,768]{1,0:T(8,128)(2,1)}) %all-gather.7.cloned.1.call-update) | async-done | bytes 75497488 | tf_op jit(solution)/shard_map/all_gather | solution.py:77
  349.5 35.7 %gather_fusion = bf16[2048,768]{1,0:T(8,128)(2,1)} fusion(bf16[49152,768]{1,0:T(8,128)(2,1)} %all-gather.7.cloned.1.call-done, s32[2048]{0:T(1024)S(1)} %broadcast_clamp_fusion.1), kind=kCustom, calls=%fused_computation | custom fusion | bytes 6299648 | tf_op jit(solution)/shard_map/jit(_take)/gather | solution.py:96
  407.7 68.4 %fusion.8 = (f32[12,2048]{1,0:T(8,128)S(1)}, f32[2048,2048,12]{1,0,2:T(8,128)}) fusion(pred[2048,2048]{0,1:T(8,128)(4,1)} %iota_compare_fusion, bf16[2048,12,64]{0,2,1:T(8,128)(2,1)} %bitcast.171, bf16[1,2048,896]{1,2,0:T(8,128)(2,1)} %copy-done.11), kind=kOutput, calls=%fused_computation.15 | convolution fusion | flops 6593421312 | bytes 209027072 | tf_op jit(solution)/shard_map/bshd,btd->bhst/dot_general | solution.py:31
  476.1 64.7 %fusion.7 = f32[12,2048]{1,0:T(8,128)S(1)} fusion(f32[2048,2048,12]{1,0,2:T(8,128)} %get-tuple-element.92, f32[12,2048]{1,0:T(8,128)S(1)} %get-tuple-element.91, pred[2048,2048]{0,1:T(8,128)(4,1)} %iota_compare_fusion), kind=kLoop, calls=%fused_computation.14 | loop fusion | flops 201302016 | bytes 205717504 | tf_op jit(solution)/shard_map/reduce_sum | solution.py:33
  540.8 72.0 %fusion.57 = bf16[64,12,2048]{2,0,1:T(8,128)(2,1)} fusion(bf16[1,2048,896]{1,2,0:T(8,128)(2,1)} %copy-done.11, f32[12,2048]{1,0:T(8,128)S(1)} %fusion.7, f32[12,2048]{1,0:T(8,128)S(1)} %get-tuple-element.91, f32[2048,2048,12]{1,0,2:T(8,128)} %get-tuple-element.92, pred[2048,2048]{0,1:T(8,128)(4,1)} %iota_compare_fusion), kind=kOutput, calls=%fused_computation.98 | convolution fusion | flops 6695682048 | bytes 209125376 | tf_op jit(solution)/shard_map/bhst,btd->bshd/dot_general | solution.py:35
  620.1 15.6 add_convert_fusion
  635.7 29.2 %convert_reduce_fusion = (f32[3072]{0:T(1024)}, bf16[2048,3072]{1,0:T(8,128)(2,1)S(1)}) fusion(bf16[2048,3072]{1,0:T(8,128)(2,1)} %add_convert_fusion, bf16[3072,768]{1,0:T(8,128)(2,1)} %all-gather.17.cloned.1.call-done, bf16[1,2048,768]{2,1,0:T(8,128)(2,1)} %param.33), kind=kOutput, calls=%fused_computation.40 | convolution fusion | flops 9820959744 | bytes 33042432 | tf_op jit(solution)/shard_map/bsd,fd->bsf/dot_general | solution.py:50
  664.9 11.3 convert_reduce_fusion.2
  689.6 108.9 %fusion.2 = (f32[12,2048]{1,0:T(8,128)}, bf16[2048,2048,12]{1,0,2:T(8,128)(2,1)}) fusion(f32[12,2048]{1,0:T(8,128)S(1)} %fusion.7, f32[12,2048]{1,0:T(8,128)S(1)} %get-tuple-element.91, f32[2048,2048,12]{1,0,2:T(8,128)} %get-tuple-element.92, pred[2048,2048]{0,1:T(8,128)(4,1)} %iota_compare_fusion, bf16[2048,12,64]{0,2,1:T(8,128)(2,1)S(1)} %bitcast.181, ...), kind=kOutput, calls=%fused_computation.8 | convolution fusion | flops 6845079552 | bytes 309886976 | tf_op jit(solution)/shard_map/bshd,btd->bhst/dot_general | solution.py:60
  798.6 74.4 %fusion.71 = bf16[2048,64]{0,1:T(8,128)(2,1)} fusion(bf16[2048,12,64]{0,2,1:T(8,128)(2,1)} %bitcast.182, f32[12,2048]{1,0:T(8,128)S(1)} %fusion.7, f32[12,2048]{1,0:T(8,128)S(1)} %get-tuple-element.91, f32[2048,2048,12]{1,0,2:T(8,128)} %get-tuple-element.92, pred[2048,2048]{0,1:T(8,128)(4,1)} %iota_compare_fusion), kind=kOutput, calls=%fused_computation.115 | convolution fusion | flops 6694240256 | bytes 209125376 | tf_op jit(solution)/shard_map/bhst,bshd->btd/dot_general | solution.py:61
  877.0 131.1 %fusion.9 = bf16[12,2048,2048]{1,2,0:T(8,128)(2,1)} fusion(bf16[2048,2048,12]{1,0,2:T(8,128)(2,1)} %get-tuple-element.97, f32[12,2048]{1,0:T(8,128)S(1)} %copy-done.15, f32[12,2048]{1,0:T(8,128)S(1)} %fusion.7, f32[12,2048]{1,0:T(8,128)S(1)} %get-tuple-element.91, f32[2048,2048,12]{1,0,2:T(8,128)} %get-tuple-element.92, pred[2048,2048]{0,1:T(8,128)(4,1)} %iota_compare_fusion), kind=kLoop, calls=%fused_computation.16 | loop fusion | flops 452984832 | bytes 407142400 | tf_op jit(solution)/shard_map/reshape.79
  1008.2 39.4 %fusion.70 = bf16[2048,64]{0,1:T(8,128)(2,1)S(1)} fusion(bf16[12,2048,2048]{1,2,0:T(8,128)(2,1)} %fusion.9, bf16[2048,12,64]{0,2,1:T(8,128)(2,1)S(1)} %bitcast.172), kind=kOutput, calls=%fused_computation.114 | convolution fusion | flops 6442582016 | bytes 104071168 | tf_op jit(solution)/shard_map/bhst,bshd->btd/dot_general | solution.py:65
  1047.7 35.0 %convolution_convert_fusion.4 = bf16[64,12,2048]{2,0,1:T(8,128)(2,1)S(1)} fusion(bf16[12,2048,2048]{1,2,0:T(8,128)(2,1)} %fusion.9, bf16[1,2048,896]{1,2,0:T(8,128)(2,1)} %copy-done.11), kind=kOutput, calls=%fused_computation.102 | convolution fusion | flops 6444023808 | bytes 104071168 | tf_op jit(solution)/shard_map/bhst,btd->bshd/dot_general | solution.py:64
  1089.8 16.1 fusion.82
  1106.0 21.2 fusion.63
  1148.4 24.4 %scatter_custom_fusion.1 = f32[8192,768]{1,0:T(8,128)} fusion(s32[2048]{0:T(1024)} %bitcast.178, f32[2048,768]{1,0:T(8,128)} %copy.66, f32[]{:T(128)} %constant.54.clone.1), kind=kCustom, calls=%fused_computation.43 | custom fusion | flops 1572864 | bytes 25166336 | tf_op jit(solution)/shard_map/scatter-add | solution.py:102
  1172.9 46.8 %broadcast_in_dim.85 = f32[49152,768]{1,0:T(8,128)} broadcast(f32[]{:T(128)} %constant.54.clone.1), dimensions={} | broadcast | bytes 150994944 | tf_op jit(solution)/shard_map/broadcast_in_dim | solution.py:101
  1219.7 266.7 %scatter_fusion = f32[49152,768]{1,0:T(8,128)} fusion(f32[49152,768]{1,0:T(8,128)} %broadcast_in_dim.85, s32[2048]{0:T(1024)S(1)} %bitcast.177, f32[2048,768]{1,0:T(8,128)} %copy.66), kind=kCustom, calls=%fused_computation.2 | custom fusion | flops 1572864 | bytes 18882560 | tf_op jit(solution)/shard_map/scatter-add | solution.py:101
  1488.6 33.3 %all-reduce.16 = (f32[768]{0:T(1024)S(1)}, f32[768]{0:T(1024)S(1)}, f32[896]{0:T(1024)S(1)}, f32[768]{0:T(1024)S(1)}, f32[768]{0:T(1024)S(1)}, /*index=5*/f32[76...) all-reduce(f32[768]{0:T(1024)S(1)} %get-tuple-element.62, ...), channel_id=4, replica_groups=mesh['fsdp'=16] {'fsdp'}, use_global_device_ids=true, to_apply=%region_16.17.clone | all-reduce | flops 8576 | bytes 68608
  1525.4 17.3 fusion.66
  1546.7 664.7 %reduce-scatter.7.cloned.1.call-done = f32[3072,768]{1,0:T(8,128)} async-done(((f32[49152,768]{1,0:T(8,128)}), f32[3072,768]{1,0:T(8,128)}) %reduce-scatter.7.cloned.1.call-update) | async-done | bytes 9437200 | tf_op jit(solution)/shard_map/reduce_scatter | solution.py:81
  (228 shorter events, 113.3 us)
Async XLA Ops:
  7.2 70.2 %all-gather.9.cloned.1.call-start = ((), (), s32[]{:S(2)}) async-start(), calls=%async_computation.7 | async-start | bytes 13369344 | tf_op jit(solution)/shard_map/all_gather | solution.py:77
  9.6 339.8 %all-gather.7.cloned.1.call-start = ((), (), s32[]{:S(2)}) async-start(), calls=%async_computation.6 | async-start | bytes 80216064 | tf_op jit(solution)/shard_map/all_gather | solution.py:77
  16.2 47.2 %copy-start.30 = (s32[1,2048]{1,0:T(1,128)S(1)}, s32[1,2048]{1,0:T(1,128)}, u32[]{:S(2)}) copy-start(s32[1,2048]{1,0:T(1,128)} %param.17) | copy-start | bytes 24580
  16.2 47.2 %copy-start.37 = (s32[1,2048]{1,0:T(1,128)S(1)}, s32[1,2048]{1,0:T(1,128)}, u32[]{:S(2)}) copy-start(s32[1,2048]{1,0:T(1,128)} %param.18) | copy-start | bytes 24580
  16.2 49.7 %copy-start.12 = (bf16[1,2048,768]{2,1,0:T(8,128)(2,1)S(1)}, bf16[1,2048,768]{2,1,0:T(8,128)(2,1)}, u32[]{:S(2)}) copy-start(bf16[1,2048,768]{2,1,0:T(8,128)(2,1)} %param.33) | copy-start | bytes 9437188
  16.2 382.7 %all-gather.11.cloned.1.call-start = ((), (), s32[]{:S(2)}) async-start(), calls=%async_computation.8 | async-start | bytes 1462272 | tf_op jit(solution)/shard_map/all_gather | solution.py:77
  17.0 595.8 %all-gather.13.cloned.1.call-start = ((), (), s32[]{:S(2)}) async-start(), calls=%async_computation.9 | async-start | bytes 1253376 | tf_op jit(solution)/shard_map/all_gather | solution.py:77
  17.7 602.3 %all-gather.15.cloned.1.call-start = ((), (), s32[]{:S(2)}) async-start(), calls=%async_computation.10 | async-start | bytes 5013504 | tf_op jit(solution)/shard_map/all_gather | solution.py:77
  19.6 616.1 %all-gather.17.cloned.1.call-start = ((), (), s32[]{:S(2)}) async-start(), calls=%async_computation.11 | async-start | bytes 5013504 | tf_op jit(solution)/shard_map/all_gather | solution.py:77
  21.4 1525.2 %reduce-scatter.13.cloned.1.call-start = ((), (), s32[]{:S(2)}) async-start(), calls=%async_computation.15 | async-start | bytes 2506752 | tf_op jit(solution)/shard_map/reduce_scatter | solution.py:81
  63.3 335.6 %copy-start.28 = (f32[768]{0:T(1024)}, f32[768]{0:T(1024)S(1)}, u32[]{:S(2)}) copy-start(f32[768]{0:T(1024)S(1)} %convert_element_type.298) | copy-start | bytes 9220
  63.3 335.6 %copy-start.39 = (f32[768]{0:T(1024)}, f32[768]{0:T(1024)S(1)}, u32[]{:S(2)}) copy-start(f32[768]{0:T(1024)S(1)} %convert_element_type.300) | copy-start | bytes 9220
  540.8 72.0 %copy-start.43 = (f32[768]{0:T(1024)S(1)}, f32[768]{0:T(1024)}, u32[]{:S(2)}) copy-start(f32[768]{0:T(1024)} %convert_element_type.313) | copy-start | bytes 9220
  619.1 61.1 %copy-start.1 = (bf16[2048,768]{0,1:T(8,128)(2,1)}, bf16[2048,768]{0,1:T(8,128)(2,1)S(1)}, u32[]{:S(2)}) copy-start(bf16[2048,768]{0,1:T(8,128)(2,1)S(1)} %get-tuple-element.94) | copy-start | bytes 9437188
  619.1 61.1 %copy-start.18 = (f32[2048]{0:T(1024)}, f32[2048]{0:T(1024)S(1)}, u32[]{:S(2)}) copy-start(f32[2048]{0:T(1024)S(1)} %broadcast_multiply_fusion) | copy-start | bytes 24580
  620.0 60.2 %copy-start.22 = (f32[2048]{0:T(1024)}, f32[2048]{0:T(1024)S(1)}, u32[]{:S(2)}) copy-start(f32[2048]{0:T(1024)S(1)} %fusion.77) | copy-start | bytes 24580
  798.6 74.4 %copy-start.9 = (bf16[1,2048,768]{1,2,0:T(8,128)(2,1)S(1)}, bf16[1,2048,768]{1,2,0:T(8,128)(2,1)}, u32[]{:S(2)}) copy-start(bf16[1,2048,768]{1,2,0:T(8,128)(2,1)} %copy-done.8) | copy-start | bytes 9437188
  798.6 74.4 %copy-start.55 = (bf16[64,12,2048]{2,0,1:T(8,128)(2,1)S(1)}, bf16[64,12,2048]{2,0,1:T(8,128)(2,1)}, u32[]{:S(2)}) copy-start(bf16[64,12,2048]{2,0,1:T(8,128)(2,1)} %fusion.57) | copy-start | bytes 9437188
  877.0 131.1 %copy-start.4 = (bf16[1,2048,768]{1,2,0:T(8,128)(2,1)S(1)}, bf16[1,2048,768]{1,2,0:T(8,128)(2,1)}, u32[]{:S(2)}) copy-start(bf16[1,2048,768]{1,2,0:T(8,128)(2,1)} %slice.18) | copy-start | bytes 9437188
  1047.6 499.0 %reduce-scatter.11.cloned.1.call-start = ((), (), s32[]{:S(2)}) async-start(), calls=%async_computation.14 | async-start | bytes 2924544 | tf_op jit(solution)/shard_map/reduce_scatter | solution.py:81
  1089.7 457.0 %reduce-scatter.15.cloned.1.call-start = ((), (), s32[]{:S(2)}) async-start(), calls=%async_computation.16 | async-start | bytes 10027008 | tf_op jit(solution)/shard_map/reduce_scatter | solution.py:81
  1105.9 440.7 %reduce-scatter.17.cloned.1.call-start = ((), (), s32[]{:S(2)}) async-start(), calls=%async_computation.17 | async-start | bytes 10027008 | tf_op jit(solution)/shard_map/reduce_scatter | solution.py:81
  1127.2 419.5 %reduce-scatter.9.cloned.1.call-start = ((), (), s32[]{:S(2)}) async-start(), calls=%async_computation.13 | async-start | bytes 26738688 | tf_op jit(solution)/shard_map/reduce_scatter | solution.py:81
  1172.8 1038.6 %reduce-scatter.7.cloned.1.call-start = ((), (), s32[]{:S(2)}) async-start(), calls=%async_computation.12 | async-start | bytes 160432128 | tf_op jit(solution)/shard_map/reduce_scatter | solution.py:81
  (46 other events, 454.9 us)
Sparse Core Ops, SparseCore 0:
  10.8 66.5 all-gather.8
  80.2 269.2 all-gather.6
  352.3 26.1 all-gather.10
  381.2 25.6 all-gather.12
  409.5 36.6 all-gather.14
  448.8 36.6 all-gather.16
  1047.7 51.6 reduce-scatter.12
  1104.3 52.9 reduce-scatter.10
  1162.6 79.4 reduce-scatter.14
  1247.2 79.4 reduce-scatter.16
  1332.0 137.7 reduce-scatter.8
  1486.5 724.8 reduce-scatter.6
where the time goes:
time: 2240 us; the launch traced here: 2220 us
  waiting for transfers between devices  928 us (41%)
  matrix products  541 us (24%)
  other arithmetic  535 us (24%)
  local copies, waits for them, and re-layouts  129 us (6%)
  blocking collectives  69.1 us (3%)
    reduce_scatter x6, waiting for transfers between devices, scatter_sum(): return lax.psum_scatter(dense_grad, 'fsdp', scatter_dimension=0, tiled=True)  665 us
    scatter-add x1, other arithmetic, device_body(): jax.ops.segment_sum(flat_dx, tokens.reshape(-1), num_segments=tok_full.sh...  267 us
    all_gather x6, waiting for transfers between devices, gather_rows(): lax.all_gather(row_shard.astype(jnp.bfloat16), 'fsdp', axis=0, tiled=True)  263 us
    another operation x1, other arithmetic  131 us
    dot_general x1, matrix products, layer_pass(): jnp.einsum('bshd,btd->bhst', d_context, value_head, preferred_element_typ...  109 us
    dot_general x1, matrix products, layer_pass(): jnp.einsum('bhst,bshd->btd', prob_lo, d_context, preferred_element_type=j...  74.4 us
    dot_general x1, matrix products, layer_pass(): jnp.einsum('bhst,btd->bshd', prob_lo, value_head, preferred_element_type=...  72 us
    unnamed x2, blocking collectives  69.1 us
  transfers between devices with their start and end apart: 12, of which 3 were waited for; matrix products, arithmetic and copies ran while one was open for 36% of the time, Pallas kernels for 0%

commit v1 on v0

v1 whole, which is shorter than its diff:
```python
import jax
import jax.numpy as jnp
from jax import lax
from jax.experimental import pallas as pl
from jax.experimental.pallas import tpu as pltpu
from jax.sharding import PartitionSpec as P

N_DEV = 16
HEAD = 64
TILE = 256
TOK_SLOTS = 192
POS_SLOTS = 144
BF = jnp.bfloat16
F32 = jnp.float32


def exchange_body(num_split, num_bcast, *refs):
    num = num_split + num_bcast
    srcs, dsts = refs[:num], refs[num:2 * num]
    send_sem, recv_sem, own_sem = refs[2 * num:]
    me = lax.axis_index('fsdp')
    barrier = pltpu.get_barrier_semaphore()
    for off in range(1, N_DEV):
        pl.semaphore_signal(barrier, inc=1, device_id=(lax.rem(me + off, N_DEV),), device_id_type=pl.DeviceIdType.MESH)
    pl.semaphore_wait(barrier, N_DEV - 1)
    copies = []
    for off in range(1, N_DEV):
        peer = lax.rem(me + off, N_DEV)
        for k in range(num):
            copy = pltpu.make_async_remote_copy(
                src_ref=srcs[k].at[peer] if k < num_split else srcs[k],
                dst_ref=dsts[k].at[me],
                send_sem=send_sem.at[k, off],
                recv_sem=recv_sem.at[k, off],
                device_id=(peer,),
                device_id_type=pl.DeviceIdType.MESH,
            )
            copy.start()
            copies.append(copy)
    own = []
    for k in range(num):
        copy = pltpu.make_async_copy(srcs[k].at[me] if k < num_split else srcs[k], dsts[k].at[me], own_sem.at[k])
        copy.start()
        own.append(copy)
    for copy in own:
        copy.wait()
    for copy in copies:
        copy.wait()


def exchange(split, bcast, cid):
    arrays = list(split) + list(bcast)
    num = len(arrays)
    outs = [jax.ShapeDtypeStruct(a.shape, a.dtype) for a in split]
    outs += [jax.ShapeDtypeStruct((N_DEV,) + a.shape, a.dtype) for a in bcast]

    def body(*refs):
        exchange_body(len(split), len(bcast), *refs)

    return pl.pallas_call(
        body,
        out_shape=outs,
        in_specs=[pl.BlockSpec(memory_space=pl.ANY)] * num,
        out_specs=[pl.BlockSpec(memory_space=pl.ANY)] * num,
        scratch_shapes=[
            pltpu.SemaphoreType.DMA((num, N_DEV)),
            pltpu.SemaphoreType.DMA((num, N_DEV)),
            pltpu.SemaphoreType.DMA((num,)),
        ],
        compiler_params=pltpu.CompilerParams(collective_id=cid, has_side_effects=True),
        name=f'exchange_{cid}',
    )(*arrays)


def nt_dot(a, b):
    return lax.dot_general(a, b, (((1,), (1,)), ((), ())), preferred_element_type=F32)


def nn_dot(a, b):
    return lax.dot_general(a, b, (((1,), (0,)), ((), ())), preferred_element_type=F32)


def attn_fwd_tile(qi, q_ref, kv_ref, c_ref, lse_ref, s_ref, p_ref):
    q = q_ref[...] * BF(0.125)
    causal = lax.broadcasted_iota(jnp.int32, (TILE, TILE), 0) >= lax.broadcasted_iota(jnp.int32, (TILE, TILE), 1)
    lse = []
    for head in range(2):
        run_max = None
        for j in range(qi + 1):
            s = nt_dot(q, kv_ref[pl.ds(j * TILE, TILE), pl.ds(head * 128, 128)])
            if j == qi:
                s = jnp.where(causal, s, -1e30)
            s_ref[head, :, pl.ds(j * TILE, TILE)] = s
            part = jnp.maximum(s[:, :128], s[:, 128:])
            run_max = part if run_max is None else jnp.maximum(run_max, part)
        row_max = jnp.max(run_max, axis=1, keepdims=True)
        run_sum = None
        for j in range(qi + 1):
            e = jnp.exp(s_ref[head, :, pl.ds(j * TILE, TILE)] - row_max)
            s_ref[head, :, pl.ds(j * TILE, TILE)] = e
            part = e[:, :128] + e[:, 128:]
            run_sum = part if run_sum is None else run_sum + part
        row_sum = jnp.sum(run_sum, axis=1, keepdims=True)
        inv = 1.0 / row_sum
        for j in range(qi + 1):
            p_ref[head, :, pl.ds(j * TILE, TILE)] = (s_ref[head, :, pl.ds(j * TILE, TILE)] * inv).astype(BF)
        lse.append(row_max + jnp.log(row_sum))
    width = (qi + 1) * TILE
    c = nn_dot(p_ref[0, :, pl.ds(0, width)], kv_ref[pl.ds(0, width), pl.ds(256, 128)])
    c += nn_dot(p_ref[1, :, pl.ds(0, width)], kv_ref[pl.ds(0, width), pl.ds(384, 128)])
    c_ref[...] = c.astype(BF)
    lane = lax.broadcasted_iota(jnp.int32, (TILE, 128), 1)
    both = jnp.where(lane == 0, lse[0], lse[1])
    lse_ref[...] = both.T[:8, :]


def attn_fwd(qkv, kv4):
    seq = qkv.shape[0]
    model = qkv.shape[1] - 2 * HEAD
    pairs, blocks = model // 128, seq // TILE

    def body(*refs):
        for qi in range(blocks):
            @pl.when(pl.program_id(1) == qi)
            def _():
                attn_fwd_tile(qi, *refs)

    return pl.pallas_call(
        body,
        grid=(pairs, blocks),
        in_specs=[
            pl.BlockSpec((TILE, 128), lambda h, i: (i, h)),
            pl.BlockSpec((seq, 512), lambda h, i: (0, 0)),
        ],
        out_specs=[
            pl.BlockSpec((TILE, 128), lambda h, i: (i, h)),
            pl.BlockSpec((8, TILE), lambda h, i: (h, i)),
        ],
        out_shape=[
            jax.ShapeDtypeStruct((seq, model), BF),
            jax.ShapeDtypeStruct((8 * pairs, seq), F32),
        ],
        scratch_shapes=[pltpu.VMEM((2, TILE, seq), F32), pltpu.VMEM((2, TILE, seq), BF)],
        compiler_params=pltpu.CompilerParams(dimension_semantics=('arbitrary', 'arbitrary')),
        cost_estimate=pl.CostEstimate(flops=16 * seq * seq * model // 2, bytes_accessed=8 * seq * model, transcendentals=6 * seq * seq),
        name='attn_fwd',
    )(qkv, kv4)


def attn_bwd_tile(qi, q_ref, dc_ref, lse_ref, kv_ref, kt_ref, dq_ref, p_ref, pb_ref, dp_ref, ds_ref, q2_ref, dc2_ref, dk_acc, dv_acc):
    q = q_ref[...] * BF(0.125)
    dc = dc_ref[...]
    first = (lax.broadcasted_iota(jnp.int32, (1, 128), 1) < HEAD).astype(F32)
    for head in range(2):
        keep = (first if head == 0 else 1.0 - first).astype(BF)
        q2_ref[pl.ds(head * TILE, TILE), :] = q * keep
        dc2_ref[pl.ds(head * TILE, TILE), :] = dc * keep
    causal = lax.broadcasted_iota(jnp.int32, (TILE, TILE), 0) <= lax.broadcasted_iota(jnp.int32, (TILE, TILE), 1)
    width = (qi + 1) * TILE
    dq_parts = []
    for head in range(2):
        cols = pl.ds(head * TILE, TILE)
        lse_row = lse_ref[pl.ds(head, 1), :]
        run = None
        for j in range(qi + 1):
            rows = pl.ds(j * TILE, TILE)
            s = nt_dot(kv_ref[rows, pl.ds(head * 128, 128)], q)
            if j == qi:
                s = jnp.where(causal, s, -1e30)
            p = jnp.exp(s - lse_row)
            p_ref[rows, cols] = p
            pb_ref[rows, cols] = p.astype(BF)
            dp = nt_dot(kv_ref[rows, pl.ds(256 + head * 128, 128)], dc).astype(BF)
            dp_ref[rows, cols] = dp
            part = jnp.sum(p * dp.astype(F32), axis=0, keepdims=True)
            run = part if run is None else run + part
        for j in range(qi + 1):
            rows = pl.ds(j * TILE, TILE)
            ds_ref[rows, cols] = (p_ref[rows, cols] * (dp_ref[rows, cols].astype(F32) - run)).astype(BF)
        dq_parts.append(nn_dot(kt_ref[:, pl.ds(0, width)], ds_ref[pl.ds(0, width), cols]))
    dq_ref[...] = jnp.concatenate(dq_parts, axis=0).T.astype(BF)
    span = pl.ds(0, width)
    dv_acc[span, :] += nn_dot(pb_ref[span, :], dc2_ref[...])
    dk_acc[span, :] += nn_dot(ds_ref[span, :], q2_ref[...])


def attn_bwd(qkv, d_context, lse, kv4, k_t):
    seq = qkv.shape[0]
    model = qkv.shape[1] - 2 * HEAD
    pairs, blocks = model // 128, seq // TILE

    def body(q_ref, dc_ref, lse_ref, kv_ref, kt_ref, dq_ref, dkv_ref, *scratch):
        dk_acc, dv_acc = scratch[-2:]
        pair, block = pl.program_id(0), pl.program_id(1)

        @pl.when((pair == 0) & (block == 0))
        def _():
            dk_acc[...] = jnp.zeros_like(dk_acc)
            dv_acc[...] = jnp.zeros_like(dv_acc)

        for qi in range(blocks):
            @pl.when(block == qi)
            def _():
                attn_bwd_tile(qi, q_ref, dc_ref, lse_ref, kv_ref, kt_ref, dq_ref, *scratch)

        @pl.when((pair == pairs - 1) & (block == blocks - 1))
        def _():
            dk = dk_acc[...]
            dv = dv_acc[...]
            lane = lax.broadcasted_iota(jnp.int32, dk.shape, 1)
            both = jnp.where(lane < HEAD, dk + pltpu.roll(dk, HEAD, 1), dv + pltpu.roll(dv, HEAD, 1))
            dkv_ref[...] = both.astype(BF)

    return pl.pallas_call(
        body,
        grid=(pairs, blocks),
        in_specs=[
            pl.BlockSpec((TILE, 128), lambda h, i: (i, h)),
            pl.BlockSpec((TILE, 128), lambda h, i: (i, h)),
            pl.BlockSpec((8, TILE), lambda h, i: (h, i)),
            pl.BlockSpec((seq, 512), lambda h, i: (0, 0)),
            pl.BlockSpec((HEAD, seq), lambda h, i: (0, 0)),
        ],
        out_specs=[
            pl.BlockSpec((TILE, 128), lambda h, i: (i, h)),
            pl.BlockSpec((seq, 128), lambda h, i: (0, 0)),
        ],
        out_shape=[
            jax.ShapeDtypeStruct((seq, model), BF),
            jax.ShapeDtypeStruct((seq, 128), BF),
        ],
        scratch_shapes=[
            pltpu.VMEM((seq, 2 * TILE), F32),
            pltpu.VMEM((seq, 2 * TILE), BF),
            pltpu.VMEM((seq, 2 * TILE), BF),
            pltpu.VMEM((seq, 2 * TILE), BF),
            pltpu.VMEM((2 * TILE, 128), BF),
            pltpu.VMEM((2 * TILE, 128), BF),
            pltpu.VMEM((seq, 128), F32),
            pltpu.VMEM((seq, 128), F32),
        ],
        compiler_params=pltpu.CompilerParams(dimension_semantics=('arbitrary', 'arbitrary')),
        cost_estimate=pl.CostEstimate(flops=40 * seq * seq * model // 2, bytes_accessed=10 * seq * model, transcendentals=6 * seq * seq),
        name='attn_bwd',
    )(qkv, d_context, lse, kv4, k_t)


def layer_norm(rows_in, ln_gain, ln_shift):
    row_mean = jnp.mean(rows_in, axis=-1, keepdims=True)
    centered = rows_in - row_mean
    row_var = jnp.mean(centered * centered, axis=-1, keepdims=True)
    return centered * lax.rsqrt(row_var + 1e-5) * ln_gain + ln_shift


def gelu_tanh(pre_act):
    return jax.nn.gelu(pre_act, approximate=True)


def tn_dot(a, b):
    return lax.dot_general(a, b, (((0,), (0,)), ((), ())), preferred_element_type=F32)


def layer_pass(x_emb, grad_out, weights):
    (ln1_gain, ln1_bias, w_qkv, b_qkv, w_out, b_out, ln2_gain, ln2_bias, w_fc, b_fc, w_proj, b_proj) = weights
    model = x_emb.shape[1]
    x_res = x_emb.astype(F32)
    ln1_out, pull_ln1 = jax.vjp(layer_norm, x_res, ln1_gain, ln1_bias)
    ln1_act = ln1_out.astype(BF)
    qkv = (nn_dot(ln1_act, w_qkv) + b_qkv).astype(BF)
    key, value = qkv[:, model:model + HEAD], qkv[:, model + HEAD:]
    zero = jnp.zeros_like(key)
    kv4 = jnp.concatenate([key, zero, zero, key, value, zero, zero, value], axis=1)
    k_t = (key * BF(0.125)).T
    context, lse = attn_fwd(qkv, kv4)
    hidden1 = (x_res + nn_dot(context, w_out) + b_out).astype(BF)
    h1_wide = hidden1.astype(F32)
    ln2_out, pull_ln2 = jax.vjp(layer_norm, h1_wide, ln2_gain, ln2_bias)
    ln2_act = ln2_out.astype(BF)
    pre_fc = (nn_dot(ln2_act, w_fc) + b_fc).astype(BF)
    gelu_val, pull_gelu = jax.vjp(gelu_tanh, pre_fc.astype(F32))
    act_fc = gelu_val.astype(BF)
    hidden_out = (h1_wide + nn_dot(act_fc, w_proj) + b_proj).astype(BF)

    dy_wide = grad_out.astype(F32)
    g_b_proj = jnp.sum(dy_wide, axis=0)
    g_w_proj = tn_dot(act_fc, grad_out)
    d_act_fc = nt_dot(grad_out, w_proj).astype(BF)
    d_pre_fc = pull_gelu(d_act_fc.astype(F32))[0].astype(BF)
    g_b_fc = jnp.sum(d_pre_fc, axis=0, dtype=F32)
    g_w_fc = tn_dot(ln2_act, d_pre_fc)
    d_ln2_act = nt_dot(d_pre_fc, w_fc).astype(BF)
    d_h1_norm, g_ln2_gain, g_ln2_bias = pull_ln2(d_ln2_act.astype(F32))
    d_hidden1 = (dy_wide + d_h1_norm).astype(BF)
    g_b_out = jnp.sum(d_hidden1, axis=0, dtype=F32)
    g_w_out = tn_dot(context, d_hidden1)
    d_context = nt_dot(d_hidden1, w_out).astype(BF)
    d_query, d_kv = attn_bwd(qkv, d_context, lse, kv4, k_t)
    d_qkv = jnp.concatenate([d_query, d_kv], axis=1)
    g_b_qkv = jnp.sum(d_qkv, axis=0, dtype=F32)
    g_w_qkv = tn_dot(ln1_act, d_qkv)
    d_ln1_act = nt_dot(d_qkv, w_qkv).astype(BF)
    d_x_norm, g_ln1_gain, g_ln1_bias = pull_ln1(d_ln1_act.astype(F32))
    d_x0 = d_hidden1.astype(F32) + d_x_norm
    vec_grads = (g_ln1_gain, g_ln1_bias, g_b_qkv, g_b_out, g_ln2_gain, g_ln2_bias, g_b_fc, g_b_proj)
    mat_grads = (g_w_qkv, g_w_out, g_w_fc, g_w_proj)
    return hidden_out, d_x0, vec_grads, mat_grads


def slots_of(ids):
    stripe = lax.rem(ids, N_DEV)
    order = jnp.arange(ids.shape[0])
    earlier = (stripe[:, None] == stripe[None, :]) & (order[None, :] < order[:, None])
    return stripe, jnp.sum(earlier.astype(jnp.int32), axis=1)


def round_place(stripe, slot, per_peer, rnd):
    local = slot - rnd * per_peer
    return jnp.where((local >= 0) & (local < per_peer), stripe * per_peer + local, -1)


def requests(place, rows, per_peer):
    total = N_DEV * per_peer
    hit = jnp.arange(total)[:, None] == place[None, :]
    return jnp.max(jnp.where(hit, rows[None, :], -1), axis=1).reshape(N_DEV, per_peer)


def one_hot(row_ids, col_ids):
    return (row_ids[:, None] == col_ids[None, :]).astype(BF)


def solution(mesh):
    vec_spec = P('fsdp')
    mat_spec = P('fsdp', None)
    act_spec = P('fsdp', None, None)
    param_specs = (vec_spec, vec_spec, mat_spec, vec_spec, mat_spec, vec_spec, vec_spec, vec_spec, mat_spec, vec_spec, mat_spec, vec_spec)
    in_specs = (mat_spec, mat_spec, mat_spec, mat_spec) + param_specs + (act_spec,)
    out_specs = (act_spec, mat_spec, mat_spec) + param_specs

    def device_body(tokens, positions, tok_table, pos_table, ln1_gain, ln1_bias, w_qkv, b_qkv, w_out, b_out, ln2_gain, ln2_bias, w_fc, b_fc, w_proj, b_proj, grad_out):
        tokens, positions, grad_out = tokens[0], positions[0], grad_out[0]
        tok_rows, model = tok_table.shape
        pos_rows = pos_table.shape[0]
        tok_sub, pos_sub = tok_rows // N_DEV, pos_rows // N_DEV

        full = [lax.all_gather(w.astype(BF), 'fsdp', axis=0, tiled=True) for w in (w_qkv, w_out, w_fc, w_proj)]

        tok_row = (tokens // tok_rows) * tok_sub + lax.rem(tokens, tok_rows) // N_DEV
        pos_row = (positions // pos_rows) * pos_sub + lax.rem(positions, pos_rows) // N_DEV
        tok_stripe, tok_slot = slots_of(tokens)
        pos_stripe, pos_slot = slots_of(positions)
        my_rounds = jnp.maximum(jnp.max(tok_slot) // TOK_SLOTS, jnp.max(pos_slot) // POS_SLOTS) + 1

        def places(rnd):
            return round_place(tok_stripe, tok_slot, TOK_SLOTS, rnd), round_place(pos_stripe, pos_slot, POS_SLOTS, rnd)

        def request_block(tok_place, pos_place):
            tok_req = requests(tok_place, tok_row, TOK_SLOTS)
            pos_req = requests(pos_place, pos_row, POS_SLOTS)
            rounds = jnp.broadcast_to(my_rounds, (N_DEV, 1))
            flat = jnp.concatenate([tok_req, pos_req, rounds], axis=1)
            return jnp.pad(flat, ((0, 0), (0, 1024 - flat.shape[1]))).reshape(N_DEV, 8, 128)

        def read_block(block):
            flat = block.reshape(N_DEV, 1024)
            tok_req = flat[:, :TOK_SLOTS].reshape(-1)
            pos_req = flat[:, TOK_SLOTS:TOK_SLOTS + POS_SLOTS].reshape(-1)
            return tok_req, pos_req, jnp.max(flat[:, TOK_SLOTS + POS_SLOTS])

        def stripes(table, sub):
            return table.astype(BF).reshape(sub, N_DEV, model).transpose(1, 0, 2)

        shards = (ln1_gain, ln1_bias, b_qkv, b_out, ln2_gain, ln2_bias, b_fc, b_proj)
        sizes = [v.shape[0] for v in shards]
        vec_block = jnp.pad(jnp.concatenate(shards), (0, 1024 - sum(sizes))).reshape(8, 128)
        tok_place, pos_place = places(0)
        tok_stripes, pos_stripes, req_in, vec_all = exchange(
            [stripes(tok_table, tok_sub), stripes(pos_table, pos_sub), request_block(tok_place, pos_place)], [vec_block], 0)
        tok_stripes = tok_stripes.reshape(tok_rows, model)
        pos_stripes = pos_stripes.reshape(pos_rows, model)
        vec_flat = vec_all.reshape(N_DEV, 1024).astype(BF).astype(F32)
        vecs, start = [], 0
        for size in sizes:
            vecs.append(vec_flat[:, start:start + size].reshape(-1))
            start += size

        tok_req0, pos_req0, rounds = read_block(req_in)
        tok_ids, pos_ids = jnp.arange(tok_rows), jnp.arange(pos_rows)
        tok_cols, pos_cols = jnp.arange(N_DEV * TOK_SLOTS), jnp.arange(N_DEV * POS_SLOTS)

        def fetch(tok_req, pos_req, tok_place, pos_place, cid):
            tok_out = nn_dot(one_hot(tok_req, tok_ids), tok_stripes).astype(BF).reshape(N_DEV, TOK_SLOTS, model)
            pos_out = nn_dot(one_hot(pos_req, pos_ids), pos_stripes).astype(BF).reshape(N_DEV, POS_SLOTS, model)
            tok_in, pos_in = exchange([tok_out, pos_out], [], cid)
            x_tok = nn_dot(one_hot(tok_place, tok_cols), tok_in.reshape(-1, model))
            x_pos = nn_dot(one_hot(pos_place, pos_cols), pos_in.reshape(-1, model))
            return x_tok + x_pos

        def more_fetch(state):
            rnd, x_sum = state
            tok_place, pos_place = places(rnd)
            (block,) = exchange([request_block(tok_place, pos_place)], [], 2)
            tok_req, pos_req, _ = read_block(block)
            return rnd + 1, x_sum + fetch(tok_req, pos_req, tok_place, pos_place, 3)

        x_sum = fetch(tok_req0, pos_req0, tok_place, pos_place, 1)
        _, x_sum = lax.while_loop(lambda state: state[0] < rounds, more_fetch, (jnp.int32(1), x_sum))
        x_emb = x_sum.astype(BF)

        weights = (vecs[0], vecs[1], full[0], vecs[2], full[1], vecs[3], vecs[4], vecs[5], full[2], vecs[6], full[3], vecs[7])
        hidden_out, d_x0, vec_grads, mat_grads = layer_pass(x_emb, grad_out, weights)
        d_rows = d_x0.astype(BF)

        vec_out = jnp.concatenate([g.reshape(N_DEV, -1) for g in vec_grads], axis=1)
        vec_out = jnp.pad(vec_out, ((0, 0), (0, 1024 - vec_out.shape[1]))).reshape(N_DEV, 8, 128)

        def give(tok_place, pos_place, extra, cid):
            tok_out = nn_dot(one_hot(tok_cols, tok_place), d_rows).astype(BF).reshape(N_DEV, TOK_SLOTS, model)
            pos_out = nn_dot(one_hot(pos_cols, pos_place), d_rows).astype(BF).reshape(N_DEV, POS_SLOTS, model)
            return exchange([tok_out, pos_out] + extra, [], cid)

        def take(tok_req, pos_req, tok_in, pos_in):
            return (nn_dot(one_hot(tok_ids, tok_req), tok_in.reshape(-1, model)),
                    nn_dot(one_hot(pos_ids, pos_req), pos_in.reshape(-1, model)))

        tok_in, pos_in, vec_in = give(tok_place, pos_place, [vec_out], 4)
        tok_sum, pos_sum = take(tok_req0, pos_req0, tok_in, pos_in)

        def more_give(state):
            rnd, tok_sum, pos_sum = state
            tok_place, pos_place = places(rnd)
            tok_in, pos_in, block = give(tok_place, pos_place, [request_block(tok_place, pos_place)], 5)
            tok_req, pos_req, _ = read_block(block)
            tok_add, pos_add = take(tok_req, pos_req, tok_in, pos_in)
            return rnd + 1, tok_sum + tok_add, pos_sum + pos_add

        _, tok_sum, pos_sum = lax.while_loop(lambda state: state[0] < rounds, more_give, (jnp.int32(1), tok_sum, pos_sum))
        tok_back, pos_back = exchange(
            [tok_sum.astype(BF).reshape(N_DEV, tok_sub, model), pos_sum.astype(BF).reshape(N_DEV, pos_sub, model)], [], 6)
        g_tok = tok_back.transpose(1, 0, 2).reshape(tok_rows, model).astype(F32)
        g_pos = pos_back.transpose(1, 0, 2).reshape(pos_rows, model).astype(F32)

        vec_sum = jnp.sum(vec_in.reshape(N_DEV, 1024), axis=0)
        g_vecs, start = [], 0
        for size in sizes:
            g_vecs.append(vec_sum[start:start + size])
            start += size
        g_mats = [lax.psum_scatter(g, 'fsdp', scatter_dimension=0, tiled=True) for g in mat_grads]
        return (hidden_out[None], g_tok, g_pos, g_vecs[0], g_vecs[1], g_mats[0], g_vecs[2], g_mats[1], g_vecs[3],
                g_vecs[4], g_vecs[5], g_mats[2], g_vecs[6], g_mats[3], g_vecs[7])

    return jax.shard_map(device_body, mesh=mesh, in_specs=in_specs, out_specs=out_specs, check_vma=False)
```

time: 2240 us -> 1050 us (0.47)
  waiting for transfers between devices: 928 us -> 0.21 us
  Pallas kernels: 0 us -> 629 us
  other arithmetic: 535 us -> 68.2 us
  matrix products: 541 us -> 240 us
  blocking collectives: 69.1 us -> 0 us
  local copies, waits for them, and re-layouts: 129 us -> 68 us
    reduce_scatter x6 -> x4, waiting for transfers between devices: 665 us -> 0.04 us  [device_body(): lax.psum_scatter(g, 'fsdp', scatter_dimension=0, tiled=True)]
    pallas_call x0 -> x6, Pallas kernels: none -> 629 us  [the longest x4 436 us: exchange(): pl.pallas_call(body, out_shape=outs, in_specs=[pl.BlockSpec(memory_space=...]
    dot_general x18 -> x20, matrix products: 541 us -> 240 us  [the longest x12 144 us: nn_dot(): lax.dot_general(a, b, (((1,), (0,)), ((), ())), preferred_element_type=F32)]
    scatter-add x2 -> x0, other arithmetic: 291 us -> none  [the longest x1 267 us: device_body(): jax.ops.segment_sum(flat_dx, tokens.reshape(-1), num_segments=tok_full.sh...]
    all_gather x6 -> x4, waiting for transfers between devices: 263 us -> 0.04 us  [device_body(): lax.all_gather(w.astype(BF), 'fsdp', axis=0, tiled=True)]
    another operation x1 -> x0, other arithmetic: 131 us -> none
    unnamed x2 -> x0, blocking collectives: 69.1 us -> none
    gather x4 -> x0, local copies, waits for them, and re-layouts: 58 us -> none  [the longest x2 40.4 us: device_body(): tok_rows = jnp.take(tok_full, tokens, axis=0)]
  transfers between devices with their start and end apart: 12 -> 8, of which waited for: 3 -> 0; matrix products, arithmetic and copies ran while one was open for 36% -> 30% of each run, Pallas kernels for 0% -> 60%
where the time goes in v1:
time: 1050 us; the launch traced here: 1040 us
  Pallas kernels  629 us (60%)
  matrix products  240 us (23%)
  other arithmetic  68.2 us (6%)
  local copies, waits for them, and re-layouts  68 us (6%)
  between operations  19.2 us (2%)
  loops' own time  18.6 us (2%)
    pallas_call x4, Pallas kernels, exchange(): pl.pallas_call(body, out_shape=outs, in_specs=[pl.BlockSpec(memory_space=...  436 us
    dot_general x12, matrix products, nn_dot(): lax.dot_general(a, b, (((1,), (0,)), ((), ())), preferred_element_type=F32)  144 us
    pallas_call x1, Pallas kernels, attn_bwd(): pl.pallas_call(body, grid=(pairs, blocks), in_specs=[pl.BlockSpec((TILE,...  124 us
    pallas_call x1, Pallas kernels, attn_fwd(): pl.pallas_call(body, grid=(pairs, blocks), in_specs=[pl.BlockSpec((TILE,...  69.5 us
    dot_general x4, matrix products, nt_dot(): lax.dot_general(a, b, (((1,), (1,)), ((), ())), preferred_element_type=F32)  51 us
    dot_general x4, matrix products, tn_dot(): lax.dot_general(a, b, (((0,), (0,)), ((), ())), preferred_element_type=F32)  45.5 us
    unnamed x160, local copies, waits for them, and re-layouts  30.9 us
  transfers between devices with their start and end apart: 8, of which 0 were waited for; matrix products, arithmetic and copies ran while one was open for 30% of the time, Pallas kernels for 60%

profile of v1, /device:TPU:0, one launch (start us, length us, event | category | flops | bytes accessed | tf_op | source)
XLA Modules:
  0.0 1044.0 jit_solution(14766191861815865241)
XLA Ops:
  50.1 81.2 %exchange_0.1 = (bf16[16,192,768]{2,1,0:T(8,128)(2,1)}, bf16[16,32,768]{2,1,0:T(8,128)(2,1)S(1)}, s32[16,8,128]{2,1,0:T(8,128)}, f32[16,8,128]{2,1,0:T(8,128)}) custom-call(bf16[16,192,768]{2,1,0:T(8,128)(2,1)} %bitcast.184, bf16[16,32,768]{2,1,0:T(8,128)(2,1)} %bitcast.197, s32[16,8,128]{2,1,0:T(8,128)} %bitcast.208, f32[8,128]{1,0:T(8,128)} %pad_bitcast_fusion.4.refs_3_), custom_call_target="tpu_custom_call" | custom-call | tf_op jit(solution)/shard_map/exchange_0/pallas_call | solution.py:60
  139.9 17.9 %fusion.91 = bf16[3072,768]{1,0:T(8,128)(2,1)} fusion(bf16[3072,768]{1,0:T(8,128)(2,1)S(1)} %bitcast.232, s32[3072]{0:T(1024)S(1)} %eq.413), kind=kOutput, calls=%fused_computation.149 | convolution fusion | flops 14507311104 | bytes 9449472 | tf_op jit(solution)/shard_map/dot_general | solution.py:80
  157.8 123.5 %exchange_1.1 = (bf16[16,192,768]{2,1,0:T(8,128)(2,1)}, bf16[16,144,768]{2,1,0:T(8,128)(2,1)}) custom-call(bf16[16,192,768]{2,1,0:T(8,128)(2,1)} %bitcast.190, bf16[16,144,768]{2,1,0:T(8,128)(2,1)} %bitcast.196), custom_call_target="tpu_custom_call" | custom-call | tf_op jit(solution)/shard_map/exchange_1/pallas_call | solution.py:60
  281.4 11.0 %fusion.54 = f32[2048,768]{1,0:T(8,128)S(1)} fusion(bf16[2304,768]{1,0:T(8,128)(2,1)} %bitcast.239, s32[2048]{0:T(1024)S(1)} %get-tuple-element.603), kind=kOutput, calls=%fused_computation.88 | convolution fusion | flops 7252475904 | bytes 9838592 | tf_op jit(solution)/shard_map/dot_general | solution.py:80
  292.4 13.2 %fusion.95 = f32[2048,768]{1,0:T(8,128)} fusion(f32[2048,768]{1,0:T(8,128)S(1)} %fusion.54, bf16[3072,768]{1,0:T(8,128)(2,1)S(1)} %bitcast.236, s32[2048]{0:T(1024)S(1)} %get-tuple-element.584), kind=kOutput, calls=%fused_computation.157 | convolution fusion | flops 9671540736 | bytes 17309696 | tf_op jit(solution)/shard_map/dot_general | solution.py:80
  305.6 11.3 %while.28 = (s32[]{:T(128)}, f32[2048,768]{1,0:T(8,128)}, s32[]{:T(128)}, s32[2048]{0:T(1024)S(1)}, s32[2048]{0:T(1024)S(1)}, /*index=5*/s32[2048]{0:T(1024)S(1)...) while((s32[]{:T(128)}, f32[2048,768]{1,0:T(8,128)}, ...), condition=%wide.region_10.11_spmd.clone.clone, body=%wide.region_7.10_spmd.clone.clone.sunk | while | flops 33280851968 | bytes 66725856 | solution.py:406
  332.5 6.6 add_convert_fusion.1
  356.2 69.5 %attn_fwd.1 = (bf16[2048,768]{1,0:T(8,128)(2,1)}, f32[48,2048]{1,0:T(8,128)}) custom-call(bf16[2048,896]{1,0:T(8,128)(2,1)} %copy.61.refs_0_.q_ref, bf16[2048,512]{1,0:T(8,128)(2,1)} %copy.62.refs_1_.kv_ref), custom_call_target="tpu_custom_call" | custom-call | flops 25769803776 | bytes 12582912 | tf_op jit(solution)/shard_map/attn_fwd/pallas_call | solution.py:128
  433.6 16.2 %add_convert_fusion = bf16[2048,3072]{1,0:T(8,128)(2,1)} fusion(f32[3072]{0:T(1024)S(1)} %add.254, bf16[768,3072]{1,0:T(8,128)(2,1)} %all-gather.9.cloned.1.call-done, bf16[2048,768]{0,1:T(8,128)(2,1)} %copy-done.2, f32[768]{0:T(1024)S(1)} %add.251, f32[768]{0:T(1024)S(1)} %mul.272, f32[2048]{0:T(1024)S(1)} %fusion.118, f32[2048]{0:T(1024)S(1)} %broadcast_multiply_fusion), kind=kOutput, calls=%fused_computation.76 | convolution fusion | flops 9685696512 | bytes 20482048 | tf_op jit(solution)/shard_map/dot_general | solution.py:80
  449.8 28.8 %convert_reduce_fusion = (f32[3072]{0:T(1024)S(1)}, bf16[2048,3072]{1,0:T(8,128)(2,1)S(1)}) fusion(bf16[2048,3072]{1,0:T(8,128)(2,1)} %add_convert_fusion, bf16[3072,768]{1,0:T(8,128)(2,1)} %all-gather.11.cloned.1.call-done, bf16[1,2048,768]{2,1,0:T(8,128)(2,1)} %param.37), kind=kOutput, calls=%fused_computation.75 | convolution fusion | flops 9820959744 | bytes 33042432 | tf_op jit(solution)/shard_map/dot_general | solution.py:76
  478.6 10.7 %convert_reduce_fusion.4 = (f32[768]{0:T(1024)S(1)}, f32[2048]{0:T(1024)S(1)}, bf16[2048,768]{0,1:T(8,128)(2,1)S(1)}) fusion(f32[768]{0:T(1024)S(1)} %mul.272, f32[2048]{0:T(1024)S(1)} %broadcast_multiply_fusion, bf16[2048,768]{0,1:T(8,128)(2,1)S(1)} %copy-done.3, bf16[2048,3072]{1,0:T(8,128)(2,1)S(1)} %get-tuple-element.601, ...), kind=kOutput, calls=%fused_computation.101 | convolution fusion | flops 9676256256 | bytes 23615488 | tf_op jit(solution)/shard_map/dot_general | solution.py:76
  502.9 6.2 convolution_convert_fusion.4.dc_ref
  509.1 124.1 %attn_bwd.1 = (bf16[2048,768]{1,0:T(8,128)(2,1)}, bf16[2048,128]{1,0:T(8,128)(2,1)}) custom-call(bf16[2048,896]{1,0:T(8,128)(2,1)} %copy.61.refs_0_.q_ref, bf16[2048,768]{1,0:T(8,128)(2,1)} %convolution_convert_fusion.4.dc_ref, f32[48,2048]{1,0:T(8,128)} %get-tuple-element.280.lse_ref, bf16[2048,512]{1,0:T(8,128)(2,1)} %copy.62.refs_1_.kv_ref, ...), custom_call_target="tpu_custom_call" | custom-call | flops 64424509440 | bytes 15728640 | tf_op jit(solution)/shard_map/attn_bwd/pallas_call | solution.py:214
  647.1 16.0 %fusion.121 = f32[768,3072]{1,0:T(8,128)} fusion(bf16[2048,3072]{1,0:T(8,128)(2,1)} %copy-done.71, bf16[2048,768]{0,1:T(8,128)(2,1)} %copy-done.2, f32[768]{0:T(1024)S(1)} %copy-done.53, f32[768]{0:T(1024)S(1)} %mul.272, f32[2048]{0:T(1024)S(1)} %fusion.118, f32[2048]{0:T(1024)S(1)} %broadcast_multiply_fusion), kind=kOutput, calls=%fused_computation.251 | convolution fusion | flops 9673113600 | bytes 25188352 | tf_op jit(solution)/shard_map/dot_general | solution.py:260
  681.0 17.2 %fusion.90 = bf16[3072,768]{1,0:T(8,128)(2,1)} fusion(bf16[2048,768]{0,1:T(8,128)(2,1)} %fusion.78, s32[2048]{0:T(1024)S(1)} %bitcast.224), kind=kOutput, calls=%fused_computation.148 | convolution fusion | flops 9672327168 | bytes 7872512 | tf_op jit(solution)/shard_map/dot_general | solution.py:80
  698.2 10.0 fusion.89
  708.2 136.0 %exchange_4.1 = (bf16[16,192,768]{2,1,0:T(8,128)(2,1)}, bf16[16,144,768]{2,1,0:T(8,128)(2,1)}, f32[16,8,128]{2,1,0:T(8,128)}) custom-call(bf16[16,192,768]{2,1,0:T(8,128)(2,1)} %bitcast.189, bf16[16,144,768]{2,1,0:T(8,128)(2,1)} %bitcast.195, f32[16,8,128]{2,1,0:T(8,128)} %bitcast.207), custom_call_target="tpu_custom_call" | custom-call | tf_op jit(solution)/shard_map/exchange_4/pallas_call | solution.py:60
  849.6 19.8 %fusion.37 = f32[3072,768]{1,0:T(8,128)} fusion(bf16[3072,768]{1,0:T(8,128)(2,1)S(1)} %bitcast.234, s32[3072]{0:T(1024)S(1)} %copy-done.40), kind=kOutput, calls=%fused_computation.62 | convolution fusion | flops 14504951808 | bytes 14168064 | tf_op jit(solution)/shard_map/dot_general | solution.py:80
  869.3 20.2 %fusion.96 = f32[3072,768]{1,0:T(8,128)} fusion(bf16[1,2048,768]{2,1,0:T(8,128)(2,1)S(1)} %copy-done.9, bf16[2048,3072]{1,0:T(8,128)(2,1)} %add_convert_fusion), kind=kOutput, calls=%fused_computation.161 | convolution fusion | flops 9726590976 | bytes 25165824 | tf_op jit(solution)/shard_map/dot_general | solution.py:260
  890.3 7.3 while.29
  898.9 6.4 convert_element_type.230
  906.3 95.2 %exchange_6.1 = (bf16[16,192,768]{2,1,0:T(8,128)(2,1)}, bf16[16,32,768]{2,1,0:T(8,128)(2,1)}) custom-call(bf16[16,192,768]{2,1,0:T(8,128)(2,1)} %bitcast.182, bf16[16,32,768]{2,1,0:T(8,128)(2,1)} %bitcast.199), custom_call_target="tpu_custom_call" | custom-call | tf_op jit(solution)/shard_map/exchange_6/pallas_call | solution.py:60
  1004.9 9.2 copy.70
  1016.3 17.2 %fusion.99 = bf16[1,2048,768]{1,2,0:T(8,128)(2,1)S(1)} fusion(f32[768]{0:T(1024)S(1)} %copy-done.51, bf16[3072,768]{1,0:T(8,128)(2,1)} %all-gather.11.cloned.1.call-done, bf16[2048,768]{0,1:T(8,128)(2,1)S(1)} %copy-done.4, bf16[2048,3072]{1,0:T(8,128)(2,1)} %add_convert_fusion), kind=kOutput, calls=%fused_computation.164 | convolution fusion | flops 9732882432 | bytes 23596032 | tf_op jit(solution)/shard_map/dot_general | solution.py:80
  (271 shorter events, 150.1 us)
Async XLA Ops:
  7.2 325.3 %all-gather.5.cloned.1.call-start = ((), (), s32[]{:S(2)}) async-start(), calls=%async_computation.4 | async-start | bytes 1462272 | tf_op jit(solution)/shard_map/all_gather | solution.py:345
  8.8 416.9 %all-gather.7.cloned.1.call-start = ((), (), s32[]{:S(2)}) async-start(), calls=%async_computation.5 | async-start | bytes 1253376 | tf_op jit(solution)/shard_map/all_gather | solution.py:345
  10.4 423.1 %all-gather.9.cloned.1.call-start = ((), (), s32[]{:S(2)}) async-start(), calls=%async_computation.6 | async-start | bytes 5013504 | tf_op jit(solution)/shard_map/all_gather | solution.py:345
  12.3 437.5 %all-gather.11.cloned.1.call-start = ((), (), s32[]{:S(2)}) async-start(), calls=%async_computation.7 | async-start | bytes 5013504 | tf_op jit(solution)/shard_map/all_gather | solution.py:345
  14.2 1022.7 %reduce-scatter.7.cloned.1.call-start = ((), (), s32[]{:S(2)}) async-start(), calls=%async_computation.9 | async-start | bytes 2506752 | tf_op jit(solution)/shard_map/reduce_scatter | solution.py:447
  135.9 21.9 %copy-start.41 = (s32[2304]{0:T(1024)}, s32[2304]{0:T(1024)S(1)}, u32[]{:S(2)}) copy-start(s32[2304]{0:T(1024)S(1)} %eq.417) | copy-start | bytes 27652
  136.0 21.9 %copy-start.39 = (s32[3072]{0:T(1024)}, s32[3072]{0:T(1024)S(1)}, u32[]{:S(2)}) copy-start(s32[3072]{0:T(1024)S(1)} %eq.413) | copy-start | bytes 36868
  324.5 101.2 %copy-start = (bf16[2048,768]{0,1:T(8,128)(2,1)}, bf16[2048,768]{0,1:T(8,128)(2,1)S(1)}, u32[]{:S(2)}) copy-start(bf16[2048,768]{0,1:T(8,128)(2,1)S(1)} %copy.60) | copy-start | bytes 9437188
  325.0 14.1 %copy-start.22 = (f32[2048]{0:T(1024)}, f32[2048]{0:T(1024)S(1)}, u32[]{:S(2)}) copy-start(f32[2048]{0:T(1024)S(1)} %broadcast_multiply_fusion.1) | copy-start | bytes 24580
  326.5 12.6 %copy-start.26 = (f32[2048]{0:T(1024)}, f32[2048]{0:T(1024)S(1)}, u32[]{:S(2)}) copy-start(f32[2048]{0:T(1024)S(1)} %fusion.117) | copy-start | bytes 24580
  326.6 12.5 %copy-start.30 = (f32[768]{0:T(1024)}, f32[768]{0:T(1024)S(1)}, u32[]{:S(2)}) copy-start(f32[768]{0:T(1024)S(1)} %mul.266) | copy-start | bytes 9220
  326.7 12.4 %copy-start.54 = (f32[768]{0:T(1024)}, f32[768]{0:T(1024)S(1)}, u32[]{:S(2)}) copy-start(f32[768]{0:T(1024)S(1)} %add.240) | copy-start | bytes 9220
  327.0 106.5 %copy-start.52 = (f32[768]{0:T(1024)}, f32[768]{0:T(1024)S(1)}, u32[]{:S(2)}) copy-start(f32[768]{0:T(1024)S(1)} %add.251) | copy-start | bytes 9220
  449.8 28.8 %copy-start.3 = (bf16[2048,768]{0,1:T(8,128)(2,1)S(1)}, bf16[2048,768]{0,1:T(8,128)(2,1)}, u32[]{:S(2)}) copy-start(bf16[2048,768]{0,1:T(8,128)(2,1)} %copy-done.2) | copy-start | bytes 9437188
  449.8 28.8 %copy-start.64 = (bf16[768,3072]{1,0:T(8,128)(2,1)S(1)}, bf16[768,3072]{1,0:T(8,128)(2,1)}, u32[]{:S(2)}) copy-start(bf16[768,3072]{1,0:T(8,128)(2,1)} %all-gather.9.cloned.1.call-done) | copy-start | bytes 14155780
  502.8 534.1 %reduce-scatter.5.cloned.1.call-start = ((), (), s32[]{:S(2)}) async-start(), calls=%async_computation.8 | async-start | bytes 2924544 | tf_op jit(solution)/shard_map/reduce_scatter | solution.py:447
  647.0 389.9 %reduce-scatter.9.cloned.1.call-start = ((), (), s32[]{:S(2)}) async-start(), calls=%async_computation.10 | async-start | bytes 10027008 | tf_op jit(solution)/shard_map/reduce_scatter | solution.py:447
  663.1 373.8 %reduce-scatter.11.cloned.1.call-start = ((), (), s32[]{:S(2)}) async-start(), calls=%async_computation.11 | async-start | bytes 10027008 | tf_op jit(solution)/shard_map/reduce_scatter | solution.py:447
  681.0 17.2 %copy-start.7 = (bf16[2048,768]{0,1:T(8,128)(2,1)S(1)}, bf16[2048,768]{0,1:T(8,128)(2,1)}, u32[]{:S(2)}) copy-start(bf16[2048,768]{0,1:T(8,128)(2,1)} %fusion.78) | copy-start | bytes 9437188
  681.0 17.2 %copy-start.46 = (s32[1,2048]{1,0:T(1,128)S(1)}, s32[1,2048]{1,0:T(1,128)}, u32[]{:S(2)}) copy-start(s32[1,2048]{1,0:T(1,128)} %copy-done.45) | copy-start | bytes 24580
  708.1 136.0 %copy-start.42 = (s32[2304]{0:T(1024)S(1)}, s32[2304]{0:T(1024)}, u32[]{:S(2)}) copy-start(s32[2304]{0:T(1024)} %copy-done.41) | copy-start | bytes 27652
  849.6 19.8 %copy-start.9 = (bf16[1,2048,768]{2,1,0:T(8,128)(2,1)S(1)}, bf16[1,2048,768]{2,1,0:T(8,128)(2,1)}, u32[]{:S(2)}) copy-start(bf16[1,2048,768]{2,1,0:T(8,128)(2,1)} %param.37) | copy-start | bytes 9437188
  1004.8 11.4 %copy-start.4 = (bf16[2048,768]{0,1:T(8,128)(2,1)S(1)}, bf16[2048,768]{0,1:T(8,128)(2,1)}, u32[]{:S(2)}) copy-start(bf16[2048,768]{0,1:T(8,128)(2,1)} %copy-done.2) | copy-start | bytes 9437188
  1004.8 11.4 %copy-start.51 = (f32[768]{0:T(1024)S(1)}, f32[768]{0:T(1024)}, u32[]{:S(2)}) copy-start(f32[768]{0:T(1024)} %add.260) | copy-start | bytes 9220
  (57 other events, 235.6 us)
Sparse Core Ops, SparseCore 0:
  10.8 29.0 all-gather.4
  42.7 71.6 all-gather.6
  116.6 122.1 all-gather.8
  241.4 70.2 all-gather.10
  502.9 64.6 reduce-scatter.6
  647.1 65.9 reduce-scatter.4
  718.4 158.1 reduce-scatter.8
  889.7 143.5 reduce-scatter.10
